TPU v7x, 32 devices: a whole 2x2x4 slice. The times are simulated.
32 devices in a mesh: pix: 8 (over z, x), frm: 4 (over y, core).
Axes of the slice: x: 2, y: 2, z: 4, core: 2. Of those that a mesh axis runs over, the one named last changes fastest.
Arguments:
- frames_y: bfloat16 [1024, 2048], P('pix', 'frm'), may hold values from -6 to 6
- traces: bfloat16 [1024, 2048], P('pix', 'frm'), may hold values from -0.13183594 to 0.13183594
- footprints: float32 [1024, 1024], P('pix'), may hold values from 0 to 2
- order: int32 [1024], replicated, may hold values from 0 to 1023, each once
- support: int32 [8, 256], P('pix'), may hold values from 0 to 1023, as said below
Outputs:
- footprints_new: float32 [1024, 1024], P('pix')
Inputs may be any that keep to these rules, and one draw needn't show every extreme that they name: `support`: row j lists 256 different neurons; it governs pixels j * 128 to (j + 1) * 128 - 1.
All inputs are finite; a program needn't handle non-finite values.
Results may differ from a plain program's by a relative error of at most 0.0003.
Values may be sent and summed in bfloat16 or wider, within the bound.
No kernel may reach another device: no remote copies, remote signals or barrier semaphores. Data moves between devices by JAX's collectives and lax.ppermute only.
A program may use at most 64 MiB of HBM per device.

v0:
```python
import jax
import jax.numpy as jnp
from jax import lax
from jax.sharding import PartitionSpec as P

BLK = 128
SWEEPS = 3


def local(frames_y, traces, footprints, order, support):
    highest = lax.Precision.HIGHEST
    pix_rows = frames_y.shape[0]
    neurons = footprints.shape[1]
    total_pixels = pix_rows * lax.axis_size("pix")
    contract = (((1,), (1,)), ((), ()))
    stacked = jnp.concatenate([frames_y, traces], axis=0)
    terms = lax.dot_general(
        stacked,
        lax.all_gather(traces, "pix", axis=0, tiled=True),
        contract,
        preferred_element_type=jnp.float32,
    )
    cross, gram_part = lax.psum((terms[:pix_rows], terms[pix_rows:]), "frm")
    gram = lax.all_gather(gram_part, "pix", axis=0, tiled=True)
    neuron_ids = lax.iota(jnp.int32, neurons)
    member = jnp.any(support[0][:, None] == neuron_ids[None, :], axis=0).astype(jnp.float32)
    keep_perm = jnp.take(member, order)
    current = jnp.take(footprints, order, axis=1)
    cross_perm = jnp.take(cross, order, axis=1)
    gram_perm = jnp.take(jnp.take(gram, order, axis=0), order, axis=1)
    diagonal = jnp.diagonal(gram_perm)
    block_count = neurons // BLK
    for sweep_index in range(SWEEPS):
        for block_index in range(block_count):
            lower = block_index * BLK
            upper = lower + BLK
            numer = cross_perm[:, lower:upper] - jnp.dot(
                current, gram_perm[:, lower:upper], precision=highest
            )
            update = keep_perm[lower:upper] * jnp.maximum(
                current[:, lower:upper] + numer / diagonal[lower:upper], 0.0
            )
            squares = lax.psum(jnp.sum(update * update, axis=0), "pix")
            scale = jnp.sqrt(squares / total_pixels + 1e-06)
            current = current.at[:, lower:upper].set(update / scale)
    return jnp.zeros_like(current).at[:, order].set(current)


def solution(mesh):
    in_specs = (P("pix", "frm"), P("pix", "frm"), P("pix", None), P(), P("pix", None))
    out_specs = P("pix", None)
    return jax.shard_map(local, mesh=mesh, in_specs=in_specs, out_specs=out_specs, check_vma=False)
```

profile of v0, /device:TPU:0, one launch (start us, length us, event | category | flops | bytes accessed | tf_op | source)
XLA Modules:
  0.0 714.0 jit_solution(11070790319049338248)
XLA Ops:
  7.3 45.2 %all-gather.3.cloned.1.call-done = bf16[1024,512]{1,0:T(8,128)(2,1)} async-done(((bf16[128,512]{1,0:T(8,128)(2,1)}), bf16[1024,512]{1,0:T(8,128)(2,1)}) %all-gather.3.cloned.1.call-update) | async-done | bytes 1048592 | tf_op jit(solution)/shard_map/all_gather | solution.py:19
  52.5 1.8 fusion.121
  54.3 1.0 fusion.128
  55.4 35.2 %all-reduce.3.cloned.1.call-done = (f32[128,1024]{1,0:T(8,128)}, f32[128,1024]{1,0:T(8,128)}) async-done(((f32[128,1024]{1,0:T(8,128)}, f32[128,1024]{1,0:T(8,128)}), (f32[128,1024]{1,0:T(8,128)}, f32[128,1024]{1,0:T(8,128)})) %all-reduce.3.cloned.1.call-update) | async-done | bytes 1048592 | tf_op jit(solution)/shard_map/psum | solution.py:23
  91.1 4.5 gather_fusion
  95.7 2.8 gather_fusion.4
  103.4 2.8 gather_fusion.5
  106.5 59.5 %all-gather.5.cloned.1.call-done = f32[1024,1024]{1,0:T(8,128)} async-done(((f32[128,1024]{1,0:T(8,128)}), f32[1024,1024]{1,0:T(8,128)}) %all-gather.5.cloned.1.call-update) | async-done | bytes 4194320 | tf_op jit(solution)/shard_map/all_gather | solution.py:24
  166.1 8.6 %gather_fusion.1 = f32[1024,1024]{1,0:T(8,128)} fusion(f32[1024,1024]{1,0:T(8,128)} %all-gather.5.cloned.1.call-done, s32[1024]{0:T(1024)S(1)} %get-tuple-element.316), kind=kCustom, calls=%fused_computation.3 | custom fusion | bytes 8392704 | tf_op jit(solution)/shard_map/jit(_take)/gather | solution.py:30
  174.7 4.5 broadcast_select_fusion
  179.2 5.3 copy.24
  184.5 8.6 %gather_fusion.2 = f32[1024,1024]{1,0:T(8,128)} fusion(f32[1024,1024]{0,1:T(8,128)} %copy.24, s32[1024]{0:T(1024)S(1)} %get-tuple-element.316), kind=kCustom, calls=%fused_computation.4 | custom fusion | bytes 8392704 | tf_op jit(solution)/shard_map/jit(_take)/gather | solution.py:30
  193.1 4.5 select_bitcast_fusion
  197.7 16.8 %gather_fusion.3 = f32[1024]{0:T(1024)S(1)} fusion(f32[1024,1024]{0,1:T(8,128)} %select_bitcast_fusion, s32[1024]{0:T(1024)S(1)} %bitcast.35), kind=kCustom, calls=%fused_computation.5 | custom fusion | bytes 16384 | tf_op jit(solution)/shard_map/jit(diagonal)/cond/branch_0_fun/gather | solution.py:31
  214.5 1.6 multiply_reduce_fusion.23
  216.1 19.0 %psum.184 = f32[128]{0:T(128)S(1)} all-reduce(f32[128]{0:T(128)S(1)} %get-tuple-element.320), channel_id=1, replica_groups=mesh['pix'=8,'frm'=4] {'pix'}, use_global_device_ids=true, to_apply=%region_5.7 | all-reduce | flops 128 | bytes 1024 | tf_op jit(solution)/shard_map/psum | solution.py:43
  235.8 1.6 multiply_reduce_fusion.22
  237.4 17.3 %psum.185 = f32[128]{0:T(128)S(1)} all-reduce(f32[128]{0:T(128)S(1)} %get-tuple-element.322), channel_id=1, replica_groups=mesh['pix'=8,'frm'=4] {'pix'}, use_global_device_ids=true, to_apply=%region_8.10 | all-reduce | flops 128 | bytes 1024 | tf_op jit(solution)/shard_map/psum | solution.py:43
  255.3 1.6 multiply_reduce_fusion.21
  257.0 19.0 %psum.186 = f32[128]{0:T(128)S(1)} all-reduce(f32[128]{0:T(128)S(1)} %get-tuple-element.324), channel_id=1, replica_groups=mesh['pix'=8,'frm'=4] {'pix'}, use_global_device_ids=true, to_apply=%region_11.13 | all-reduce | flops 128 | bytes 1024 | tf_op jit(solution)/shard_map/psum | solution.py:43
  276.7 1.6 multiply_reduce_fusion.20
  278.3 17.2 %psum.187 = f32[128]{0:T(128)S(1)} all-reduce(f32[128]{0:T(128)S(1)} %get-tuple-element.326), channel_id=1, replica_groups=mesh['pix'=8,'frm'=4] {'pix'}, use_global_device_ids=true, to_apply=%region_14.16 | all-reduce | flops 128 | bytes 1024 | tf_op jit(solution)/shard_map/psum | solution.py:43
  296.2 1.6 multiply_reduce_fusion.19
  297.8 19.0 %psum.188 = f32[128]{0:T(128)S(1)} all-reduce(f32[128]{0:T(128)S(1)} %get-tuple-element.328), channel_id=1, replica_groups=mesh['pix'=8,'frm'=4] {'pix'}, use_global_device_ids=true, to_apply=%region_17.19 | all-reduce | flops 128 | bytes 1024 | tf_op jit(solution)/shard_map/psum | solution.py:43
  317.5 1.6 multiply_reduce_fusion.18
  319.1 17.2 %psum.189 = f32[128]{0:T(128)S(1)} all-reduce(f32[128]{0:T(128)S(1)} %get-tuple-element.330), channel_id=1, replica_groups=mesh['pix'=8,'frm'=4] {'pix'}, use_global_device_ids=true, to_apply=%region_20.22 | all-reduce | flops 128 | bytes 1024 | tf_op jit(solution)/shard_map/psum | solution.py:43
  337.0 1.6 multiply_reduce_fusion.17
  338.6 19.0 %psum.190 = f32[128]{0:T(128)S(1)} all-reduce(f32[128]{0:T(128)S(1)} %get-tuple-element.332), channel_id=1, replica_groups=mesh['pix'=8,'frm'=4] {'pix'}, use_global_device_ids=true, to_apply=%region_23.25 | all-reduce | flops 128 | bytes 1024 | tf_op jit(solution)/shard_map/psum | solution.py:43
  358.3 1.6 multiply_reduce_fusion.16
  360.0 17.2 %psum.191 = f32[128]{0:T(128)S(1)} all-reduce(f32[128]{0:T(128)S(1)} %get-tuple-element.334), channel_id=1, replica_groups=mesh['pix'=8,'frm'=4] {'pix'}, use_global_device_ids=true, to_apply=%region_25.27 | all-reduce | flops 128 | bytes 1024 | tf_op jit(solution)/shard_map/psum | solution.py:43
  377.3 1.6 multiply_reduce_fusion.15
  378.9 19.0 %psum.192 = f32[128]{0:T(128)S(1)} all-reduce(f32[128]{0:T(128)S(1)} %get-tuple-element.336), channel_id=1, replica_groups=mesh['pix'=8,'frm'=4] {'pix'}, use_global_device_ids=true, to_apply=%region_27.29 | all-reduce | flops 128 | bytes 1024 | tf_op jit(solution)/shard_map/psum | solution.py:43
  398.6 1.6 multiply_reduce_fusion.14
  400.3 17.4 %psum.193 = f32[128]{0:T(128)S(1)} all-reduce(f32[128]{0:T(128)S(1)} %get-tuple-element.338), channel_id=1, replica_groups=mesh['pix'=8,'frm'=4] {'pix'}, use_global_device_ids=true, to_apply=%region_29.31 | all-reduce | flops 128 | bytes 1024 | tf_op jit(solution)/shard_map/psum | solution.py:43
  418.3 1.6 multiply_reduce_fusion.13
  419.9 19.0 %psum.194 = f32[128]{0:T(128)S(1)} all-reduce(f32[128]{0:T(128)S(1)} %get-tuple-element.340), channel_id=1, replica_groups=mesh['pix'=8,'frm'=4] {'pix'}, use_global_device_ids=true, to_apply=%region_31.33 | all-reduce | flops 128 | bytes 1024 | tf_op jit(solution)/shard_map/psum | solution.py:43
  439.6 1.6 multiply_reduce_fusion.12
  441.3 17.2 %psum.195 = f32[128]{0:T(128)S(1)} all-reduce(f32[128]{0:T(128)S(1)} %get-tuple-element.342), channel_id=1, replica_groups=mesh['pix'=8,'frm'=4] {'pix'}, use_global_device_ids=true, to_apply=%region_33.35 | all-reduce | flops 128 | bytes 1024 | tf_op jit(solution)/shard_map/psum | solution.py:43
  459.1 1.6 multiply_reduce_fusion.11
  460.8 19.0 %psum.196 = f32[128]{0:T(128)S(1)} all-reduce(f32[128]{0:T(128)S(1)} %get-tuple-element.344), channel_id=1, replica_groups=mesh['pix'=8,'frm'=4] {'pix'}, use_global_device_ids=true, to_apply=%region_35.37 | all-reduce | flops 128 | bytes 1024 | tf_op jit(solution)/shard_map/psum | solution.py:43
  480.5 1.6 multiply_reduce_fusion.10
  482.1 17.2 %psum.197 = f32[128]{0:T(128)S(1)} all-reduce(f32[128]{0:T(128)S(1)} %get-tuple-element.346), channel_id=1, replica_groups=mesh['pix'=8,'frm'=4] {'pix'}, use_global_device_ids=true, to_apply=%region_37.39 | all-reduce | flops 128 | bytes 1024 | tf_op jit(solution)/shard_map/psum | solution.py:43
  499.9 1.6 multiply_reduce_fusion.9
  501.5 19.0 %psum.198 = f32[128]{0:T(128)S(1)} all-reduce(f32[128]{0:T(128)S(1)} %get-tuple-element.348), channel_id=1, replica_groups=mesh['pix'=8,'frm'=4] {'pix'}, use_global_device_ids=true, to_apply=%region_39.41 | all-reduce | flops 128 | bytes 1024 | tf_op jit(solution)/shard_map/psum | solution.py:43
  521.3 1.6 multiply_reduce_fusion.8
  522.9 17.2 %psum.199 = f32[128]{0:T(128)S(1)} all-reduce(f32[128]{0:T(128)S(1)} %get-tuple-element.350), channel_id=1, replica_groups=mesh['pix'=8,'frm'=4] {'pix'}, use_global_device_ids=true, to_apply=%region_41.43 | all-reduce | flops 128 | bytes 1024 | tf_op jit(solution)/shard_map/psum | solution.py:43
  540.2 1.6 multiply_reduce_fusion.7
  541.8 19.0 %psum.200 = f32[128]{0:T(128)S(1)} all-reduce(f32[128]{0:T(128)S(1)} %get-tuple-element.352), channel_id=1, replica_groups=mesh['pix'=8,'frm'=4] {'pix'}, use_global_device_ids=true, to_apply=%region_43.45 | all-reduce | flops 128 | bytes 1024 | tf_op jit(solution)/shard_map/psum | solution.py:43
  561.6 1.6 multiply_reduce_fusion.6
  563.2 17.3 %psum.201 = f32[128]{0:T(128)S(1)} all-reduce(f32[128]{0:T(128)S(1)} %get-tuple-element.354), channel_id=1, replica_groups=mesh['pix'=8,'frm'=4] {'pix'}, use_global_device_ids=true, to_apply=%region_45.47 | all-reduce | flops 128 | bytes 1024 | tf_op jit(solution)/shard_map/psum | solution.py:43
  581.1 1.6 multiply_reduce_fusion.5
  582.7 19.0 %psum.202 = f32[128]{0:T(128)S(1)} all-reduce(f32[128]{0:T(128)S(1)} %get-tuple-element.356), channel_id=1, replica_groups=mesh['pix'=8,'frm'=4] {'pix'}, use_global_device_ids=true, to_apply=%region_47.49 | all-reduce | flops 128 | bytes 1024 | tf_op jit(solution)/shard_map/psum | solution.py:43
  602.4 1.6 multiply_reduce_fusion.4
  604.0 17.3 %psum.203 = f32[128]{0:T(128)S(1)} all-reduce(f32[128]{0:T(128)S(1)} %get-tuple-element.358), channel_id=1, replica_groups=mesh['pix'=8,'frm'=4] {'pix'}, use_global_device_ids=true, to_apply=%region_49.51 | all-reduce | flops 128 | bytes 1024 | tf_op jit(solution)/shard_map/psum | solution.py:43
  621.9 1.6 multiply_reduce_fusion.3
  623.6 19.0 %psum.204 = f32[128]{0:T(128)S(1)} all-reduce(f32[128]{0:T(128)S(1)} %get-tuple-element.360), channel_id=1, replica_groups=mesh['pix'=8,'frm'=4] {'pix'}, use_global_device_ids=true, to_apply=%region_51.53 | all-reduce | flops 128 | bytes 1024 | tf_op jit(solution)/shard_map/psum | solution.py:43
  643.2 1.6 multiply_reduce_fusion.2
  644.9 17.3 %psum.205 = f32[128]{0:T(128)S(1)} all-reduce(f32[128]{0:T(128)S(1)} %get-tuple-element.362), channel_id=1, replica_groups=mesh['pix'=8,'frm'=4] {'pix'}, use_global_device_ids=true, to_apply=%region_53.55 | all-reduce | flops 128 | bytes 1024 | tf_op jit(solution)/shard_map/psum | solution.py:43
  662.7 1.6 multiply_reduce_fusion.1
  664.4 19.0 %psum.206 = f32[128]{0:T(128)S(1)} all-reduce(f32[128]{0:T(128)S(1)} %get-tuple-element.364), channel_id=1, replica_groups=mesh['pix'=8,'frm'=4] {'pix'}, use_global_device_ids=true, to_apply=%region_55.57 | all-reduce | flops 128 | bytes 1024 | tf_op jit(solution)/shard_map/psum | solution.py:43
  684.1 1.6 multiply_reduce_fusion
  685.7 17.3 %psum.207 = f32[128]{0:T(128)S(1)} all-reduce(f32[128]{0:T(128)S(1)} %get-tuple-element.366), channel_id=1, replica_groups=mesh['pix'=8,'frm'=4] {'pix'}, use_global_device_ids=true, to_apply=%region_57.59 | all-reduce | flops 128 | bytes 1024 | tf_op jit(solution)/shard_map/psum | solution.py:43
  703.2 3.2 scatter_custom_fusion
  706.4 1.0 copy.26
  (81 shorter events, 20.2 us)
Async XLA Ops:
  6.5 84.1 %copy-start.3 = (s32[1,256]{1,0:T(1,128)S(1)}, s32[1,256]{1,0:T(1,128)}, u32[]{:S(2)}) copy-start(s32[1,256]{1,0:T(1,128)} %param.59) | copy-start | bytes 3076
  6.5 84.3 %copy-start = (f32[128,1024]{1,0:T(8,128)S(1)}, f32[128,1024]{1,0:T(8,128)}, u32[]{:S(2)}) copy-start(f32[128,1024]{1,0:T(8,128)} %param.57) | copy-start | bytes 1572868
  6.5 84.5 %copy-start.2 = (s32[1024]{0:T(1024)S(1)}, s32[1024]{0:T(1024)}, u32[]{:S(2)}) copy-start(s32[1024]{0:T(1024)} %param.58) | copy-start | bytes 12292
  6.5 46.0 %all-gather.3.cloned.1.call-start = ((), (), s32[]{:S(2)}) async-start(), calls=%async_computation | async-start | bytes 1179648 | tf_op jit(solution)/shard_map/all_gather | solution.py:19
  7.3 83.4 %all-reduce.3.cloned.1.call-start = ((), (), s32[]{:S(2)}) async-start(), calls=%async_computation.2 | async-start | bytes 2097152 | tf_op jit(solution)/shard_map/psum | solution.py:23
  55.4 110.7 %all-gather.5.cloned.1.call-start = ((), (), s32[]{:S(2)}) async-start(), calls=%async_computation.1 | async-start | bytes 4718592 | tf_op jit(solution)/shard_map/all_gather | solution.py:24
  91.1 12.1 %copy-start.1 = (f32[128,1024]{1,0:T(8,128)S(1)}, f32[128,1024]{1,0:T(8,128)}, u32[]{:S(2)}) copy-start(f32[128,1024]{1,0:T(8,128)} %get-tuple-element.295) | copy-start | bytes 1572868
Sparse Core Ops, SparseCore 0:
  9.5 42.9 all-gather.2
  55.5 35.0 all-reduce.2
  92.7 73.2 all-gather.4
where the time goes:
time: 717 us; the launch traced here: 714 us
  blocking collectives  435 us (61%)
  waiting for transfers between devices  141 us (20%)
  local copies, waits for them, and re-layouts  55.8 us (8%)
  matrix products  41.3 us (6%)
  other arithmetic  27.4 us (4%)
  between operations  13.5 us (2%)
    psum x24, blocking collectives, local(): squares = lax.psum(jnp.sum(update * update, axis=0), 'pix')  435 us
    all_gather x1, waiting for transfers between devices, local(): gram = lax.all_gather(gram_part, 'pix', axis=0, tiled=True)  59.5 us
    all_gather x1, waiting for transfers between devices, local(): lax.all_gather(traces, 'pix', axis=0, tiled=True)  45.2 us
    dot_general x24, matrix products, local(): jnp.dot(current, gram_perm[:, lower:upper], precision=highest)  39.5 us
    psum x1, waiting for transfers between devices, local(): cross, gram_part = lax.psum((terms[:pix_rows], terms[pix_rows:]), 'frm')  35.2 us
    gather x2, local copies, waits for them, and re-layouts, local(): gram_perm = jnp.take(jnp.take(gram, order, axis=0), order, axis=1)  17.2 us
    gather x1, local copies, waits for them, and re-layouts, local(): diagonal = jnp.diagonal(gram_perm)  16.8 us
  transfers between devices with their start and end apart: 3, of which 3 were waited for; matrix products, arithmetic and copies ran while one was open for 2% of the time, Pallas kernels for 0%

commit v1 on v0

--- a/solution.py
+++ b/solution.py
@@ -5,6 +5,21 @@
 
 BLK = 128
 SWEEPS = 3
+
+
+def balance_waves_here(block_here):
+    axis_len = lax.axis_size("pix")
+    w_next = [(i0 - 1, i0) for i0 in range(1, axis_len)] + [(axis_len - 1, 0)]
+    n_now = block_here
+    buffers = [n_now]
+    for _ in tuple(range(axis_len - 1)):
+        n_now = lax.ppermute(n_now, "pix", w_next)
+        buffers += [n_now]
+    return jnp.roll(
+        jnp.concatenate([*reversed(buffers)], axis=0),
+        shift=(lax.axis_index("pix") + 1) * n_now.shape[0],
+        axis=0,
+    )
 
 
 def local(frames_y, traces, footprints, order, support):
@@ -21,7 +36,7 @@
         preferred_element_type=jnp.float32,
     )
     cross, gram_part = lax.psum((terms[:pix_rows], terms[pix_rows:]), "frm")
-    gram = lax.all_gather(gram_part, "pix", axis=0, tiled=True)
+    gram = balance_waves_here(gram_part)
     neuron_ids = lax.iota(jnp.int32, neurons)
     member = jnp.any(support[0][:, None] == neuron_ids[None, :], axis=0).astype(jnp.float32)
     keep_perm = jnp.take(member, order)

time: 717 us -> 757 us (1.056)
  waiting for transfers between devices: 141 us -> 164 us
  local copies, waits for them, and re-layouts: 55.8 us -> 67.6 us
    ppermute x0 -> x7, waiting for transfers between devices: none -> 82.4 us  [balance_waves_here(): n_now = lax.ppermute(n_now, 'pix', w_next)]
    all_gather x1 -> x0, waiting for transfers between devices: 59.5 us -> none  [local(): gram = lax.all_gather(gram_part, 'pix', axis=0, tiled=True)]
  transfers between devices with their start and end apart: 3 -> 9, of which waited for: 3 -> 8; matrix products, arithmetic and copies ran while one was open for 2% -> 3% of each run, Pallas kernels for 0% -> 0%
where the time goes in v1:
time: 757 us; the launch traced here: 754 us
  blocking collectives  438 us (58%)
  waiting for transfers between devices  164 us (22%)
  local copies, waits for them, and re-layouts  67.6 us (9%)
  matrix products  41.3 us (5%)
  other arithmetic  28.5 us (4%)
  between operations  13.9 us (2%)
    psum x24, blocking collectives, local(): squares = lax.psum(jnp.sum(update * update, axis=0), 'pix')  438 us
    ppermute x7, waiting for transfers between devices, balance_waves_here(): n_now = lax.ppermute(n_now, 'pix', w_next)  82.4 us
    all_gather x1, waiting for transfers between devices, local(): lax.all_gather(traces, 'pix', axis=0, tiled=True)  45.2 us
    dot_general x24, matrix products, local(): jnp.dot(current, gram_perm[:, lower:upper], precision=highest)  39.5 us
    psum x1, waiting for transfers between devices, local(): cross, gram_part = lax.psum((terms[:pix_rows], terms[pix_rows:]), 'frm')  35.2 us
    gather x2, local copies, waits for them, and re-layouts, local(): gram_perm = jnp.take(jnp.take(gram, order, axis=0), order, axis=1)  17.2 us
    gather x1, local copies, waits for them, and re-layouts, local(): diagonal = jnp.diagonal(gram_perm)  16.8 us
  transfers between devices with their start and end apart: 9, of which 8 were waited for; matrix products, arithmetic and copies ran while one was open for 3% of the time, Pallas kernels for 0%

profile of v1, /device:TPU:0, one launch (start us, length us, event | category | flops | bytes accessed | tf_op | source)
XLA Modules:
  0.0 754.5 jit_solution(16506689867636812199)
XLA Ops:
  7.3 45.2 %all-gather.2.cloned.1.call-done = bf16[1024,512]{1,0:T(8,128)(2,1)} async-done(((bf16[128,512]{1,0:T(8,128)(2,1)}), bf16[1024,512]{1,0:T(8,128)(2,1)}) %all-gather.2.cloned.1.call-update) | async-done | bytes 1048592 | tf_op jit(solution)/shard_map/all_gather | solution.py:34
  52.5 1.8 fusion.121
  55.4 35.2 %all-reduce.3.cloned.1.call-done = (f32[128,1024]{1,0:T(8,128)}, f32[128,1024]{1,0:T(8,128)}) async-done(((f32[128,1024]{1,0:T(8,128)}, f32[128,1024]{1,0:T(8,128)}), (f32[128,1024]{1,0:T(8,128)}, f32[128,1024]{1,0:T(8,128)})) %all-reduce.3.cloned.1.call-update) | async-done | bytes 1048592 | tf_op jit(solution)/shard_map/psum | solution.py:38
  92.1 14.8 %collective-permute-done = f32[128,1024]{1,0:T(8,128)S(1)} collective-permute-done((f32[128,1024]{1,0:T(8,128)}, f32[128,1024]{1,0:T(8,128)S(1)}, u32[]{:S(2)}, u32[]{:S(2)}) %collective-permute-start) | collective-permute-done | bytes 524320 | tf_op jit(solution)/shard_map/ppermute | solution.py:16
  106.9 15.2 %collective-permute-done.1 = f32[128,1024]{1,0:T(8,128)S(1)} collective-permute-done((f32[128,1024]{1,0:T(8,128)S(1)}, f32[128,1024]{1,0:T(8,128)S(1)}, u32[]{:S(2)}, u32[]{:S(2)}) %collective-permute-start.1) | collective-permute-done | bytes 524320 | tf_op jit(solution)/shard_map/ppermute | solution.py:16
  122.1 14.3 %collective-permute-done.2 = f32[128,1024]{1,0:T(8,128)S(1)} collective-permute-done((f32[128,1024]{1,0:T(8,128)S(1)}, f32[128,1024]{1,0:T(8,128)S(1)}, u32[]{:S(2)}, u32[]{:S(2)}) %collective-permute-start.2) | collective-permute-done | bytes 524320 | tf_op jit(solution)/shard_map/ppermute | solution.py:16
  136.4 13.5 %collective-permute-done.3 = f32[128,1024]{1,0:T(8,128)S(1)} collective-permute-done((f32[128,1024]{1,0:T(8,128)S(1)}, f32[128,1024]{1,0:T(8,128)S(1)}, u32[]{:S(2)}, u32[]{:S(2)}) %collective-permute-start.3) | collective-permute-done | bytes 524320 | tf_op jit(solution)/shard_map/ppermute | solution.py:16
  149.9 12.6 %collective-permute-done.4 = f32[128,1024]{1,0:T(8,128)S(1)} collective-permute-done((f32[128,1024]{1,0:T(8,128)S(1)}, f32[128,1024]{1,0:T(8,128)S(1)}, u32[]{:S(2)}, u32[]{:S(2)}) %collective-permute-start.4) | collective-permute-done | bytes 524320 | tf_op jit(solution)/shard_map/ppermute | solution.py:16
  162.7 12.0 %collective-permute-done.5 = f32[128,1024]{1,0:T(8,128)} collective-permute-done((f32[128,1024]{1,0:T(8,128)S(1)}, f32[128,1024]{1,0:T(8,128)}, u32[]{:S(2)}, u32[]{:S(2)}) %collective-permute-start.5) | collective-permute-done | bytes 524320 | tf_op jit(solution)/shard_map/ppermute | solution.py:16
  176.1 4.5 gather_fusion
  180.6 2.8 gather_fusion.4
  190.2 2.8 gather_fusion.5
  201.4 2.2 constant_dynamic-slice_fusion
  203.6 8.6 %gather_fusion.1 = f32[1024,1024]{1,0:T(8,128)} fusion(f32[1024,1024]{1,0:T(8,128)} %constant_dynamic-slice_fusion, s32[1024]{0:T(1024)S(1)} %get-tuple-element.316), kind=kCustom, calls=%fused_computation.3 | custom fusion | bytes 8392704 | tf_op jit(solution)/shard_map/jit(_take)/gather | solution.py:45
  212.3 4.5 broadcast_select_fusion
  216.8 5.3 copy.24
  222.1 8.6 %gather_fusion.2 = f32[1024,1024]{1,0:T(8,128)} fusion(f32[1024,1024]{0,1:T(8,128)} %copy.24, s32[1024]{0:T(1024)S(1)} %get-tuple-element.316), kind=kCustom, calls=%fused_computation.4 | custom fusion | bytes 8392704 | tf_op jit(solution)/shard_map/jit(_take)/gather | solution.py:45
  230.7 4.5 select_bitcast_fusion
  235.2 16.8 %gather_fusion.3 = f32[1024]{0:T(1024)S(1)} fusion(f32[1024,1024]{0,1:T(8,128)} %select_bitcast_fusion, s32[1024]{0:T(1024)S(1)} %bitcast.35), kind=kCustom, calls=%fused_computation.5 | custom fusion | bytes 16384 | tf_op jit(solution)/shard_map/jit(diagonal)/cond/branch_0_fun/gather | solution.py:46
  252.1 1.6 multiply_reduce_fusion.23
  253.7 21.8 %psum.184 = f32[128]{0:T(128)S(1)} all-reduce(f32[128]{0:T(128)S(1)} %get-tuple-element.320), channel_id=1, replica_groups=mesh['pix'=8,'frm'=4] {'pix'}, use_global_device_ids=true, to_apply=%region_5.7 | all-reduce | flops 128 | bytes 1024 | tf_op jit(solution)/shard_map/psum | solution.py:58
  276.2 1.6 multiply_reduce_fusion.22
  277.8 17.1 %psum.185 = f32[128]{0:T(128)S(1)} all-reduce(f32[128]{0:T(128)S(1)} %get-tuple-element.322), channel_id=1, replica_groups=mesh['pix'=8,'frm'=4] {'pix'}, use_global_device_ids=true, to_apply=%region_8.10 | all-reduce | flops 128 | bytes 1024 | tf_op jit(solution)/shard_map/psum | solution.py:58
  295.6 1.6 multiply_reduce_fusion.21
  297.2 19.1 %psum.186 = f32[128]{0:T(128)S(1)} all-reduce(f32[128]{0:T(128)S(1)} %get-tuple-element.324), channel_id=1, replica_groups=mesh['pix'=8,'frm'=4] {'pix'}, use_global_device_ids=true, to_apply=%region_11.13 | all-reduce | flops 128 | bytes 1024 | tf_op jit(solution)/shard_map/psum | solution.py:58
  317.0 1.6 multiply_reduce_fusion.20
  318.6 17.1 %psum.187 = f32[128]{0:T(128)S(1)} all-reduce(f32[128]{0:T(128)S(1)} %get-tuple-element.326), channel_id=1, replica_groups=mesh['pix'=8,'frm'=4] {'pix'}, use_global_device_ids=true, to_apply=%region_14.16 | all-reduce | flops 128 | bytes 1024 | tf_op jit(solution)/shard_map/psum | solution.py:58
  336.4 1.6 multiply_reduce_fusion.19
  338.1 19.2 %psum.188 = f32[128]{0:T(128)S(1)} all-reduce(f32[128]{0:T(128)S(1)} %get-tuple-element.328), channel_id=1, replica_groups=mesh['pix'=8,'frm'=4] {'pix'}, use_global_device_ids=true, to_apply=%region_17.19 | all-reduce | flops 128 | bytes 1024 | tf_op jit(solution)/shard_map/psum | solution.py:58
  357.8 1.6 multiply_reduce_fusion.18
  359.4 17.1 %psum.189 = f32[128]{0:T(128)S(1)} all-reduce(f32[128]{0:T(128)S(1)} %get-tuple-element.330), channel_id=1, replica_groups=mesh['pix'=8,'frm'=4] {'pix'}, use_global_device_ids=true, to_apply=%region_20.22 | all-reduce | flops 128 | bytes 1024 | tf_op jit(solution)/shard_map/psum | solution.py:58
  377.3 1.6 multiply_reduce_fusion.17
  378.9 19.3 %psum.190 = f32[128]{0:T(128)S(1)} all-reduce(f32[128]{0:T(128)S(1)} %get-tuple-element.332), channel_id=1, replica_groups=mesh['pix'=8,'frm'=4] {'pix'}, use_global_device_ids=true, to_apply=%region_23.25 | all-reduce | flops 128 | bytes 1024 | tf_op jit(solution)/shard_map/psum | solution.py:58
  398.9 1.6 multiply_reduce_fusion.16
  400.6 17.1 %psum.191 = f32[128]{0:T(128)S(1)} all-reduce(f32[128]{0:T(128)S(1)} %get-tuple-element.334), channel_id=1, replica_groups=mesh['pix'=8,'frm'=4] {'pix'}, use_global_device_ids=true, to_apply=%region_25.27 | all-reduce | flops 128 | bytes 1024 | tf_op jit(solution)/shard_map/psum | solution.py:58
  419.4 19.1 %psum.192 = f32[128]{0:T(128)S(1)} all-reduce(f32[128]{0:T(128)S(1)} %get-tuple-element.336), channel_id=1, replica_groups=mesh['pix'=8,'frm'=4] {'pix'}, use_global_device_ids=true, to_apply=%region_27.29 | all-reduce | flops 128 | bytes 1024 | tf_op jit(solution)/shard_map/psum | solution.py:58
  439.1 1.6 multiply_reduce_fusion.14
  440.8 17.1 %psum.193 = f32[128]{0:T(128)S(1)} all-reduce(f32[128]{0:T(128)S(1)} %get-tuple-element.338), channel_id=1, replica_groups=mesh['pix'=8,'frm'=4] {'pix'}, use_global_device_ids=true, to_apply=%region_29.31 | all-reduce | flops 128 | bytes 1024 | tf_op jit(solution)/shard_map/psum | solution.py:58
  458.6 1.6 multiply_reduce_fusion.13
  460.2 19.1 %psum.194 = f32[128]{0:T(128)S(1)} all-reduce(f32[128]{0:T(128)S(1)} %get-tuple-element.340), channel_id=1, replica_groups=mesh['pix'=8,'frm'=4] {'pix'}, use_global_device_ids=true, to_apply=%region_31.33 | all-reduce | flops 128 | bytes 1024 | tf_op jit(solution)/shard_map/psum | solution.py:58
  481.6 17.1 %psum.195 = f32[128]{0:T(128)S(1)} all-reduce(f32[128]{0:T(128)S(1)} %get-tuple-element.342), channel_id=1, replica_groups=mesh['pix'=8,'frm'=4] {'pix'}, use_global_device_ids=true, to_apply=%region_33.35 | all-reduce | flops 128 | bytes 1024 | tf_op jit(solution)/shard_map/psum | solution.py:58
  501.0 19.1 %psum.196 = f32[128]{0:T(128)S(1)} all-reduce(f32[128]{0:T(128)S(1)} %get-tuple-element.344), channel_id=1, replica_groups=mesh['pix'=8,'frm'=4] {'pix'}, use_global_device_ids=true, to_apply=%region_35.37 | all-reduce | flops 128 | bytes 1024 | tf_op jit(solution)/shard_map/psum | solution.py:58
  522.4 17.1 %psum.197 = f32[128]{0:T(128)S(1)} all-reduce(f32[128]{0:T(128)S(1)} %get-tuple-element.346), channel_id=1, replica_groups=mesh['pix'=8,'frm'=4] {'pix'}, use_global_device_ids=true, to_apply=%region_37.39 | all-reduce | flops 128 | bytes 1024 | tf_op jit(solution)/shard_map/psum | solution.py:58
  540.2 1.6 multiply_reduce_fusion.9
  541.9 19.1 %psum.198 = f32[128]{0:T(128)S(1)} all-reduce(f32[128]{0:T(128)S(1)} %get-tuple-element.348), channel_id=1, replica_groups=mesh['pix'=8,'frm'=4] {'pix'}, use_global_device_ids=true, to_apply=%region_39.41 | all-reduce | flops 128 | bytes 1024 | tf_op jit(solution)/shard_map/psum | solution.py:58
  561.6 1.6 multiply_reduce_fusion.8
  563.3 17.1 %psum.199 = f32[128]{0:T(128)S(1)} all-reduce(f32[128]{0:T(128)S(1)} %get-tuple-element.350), channel_id=1, replica_groups=mesh['pix'=8,'frm'=4] {'pix'}, use_global_device_ids=true, to_apply=%region_41.43 | all-reduce | flops 128 | bytes 1024 | tf_op jit(solution)/shard_map/psum | solution.py:58
  580.5 1.6 multiply_reduce_fusion.7
  582.1 19.1 %psum.200 = f32[128]{0:T(128)S(1)} all-reduce(f32[128]{0:T(128)S(1)} %get-tuple-element.352), channel_id=1, replica_groups=mesh['pix'=8,'frm'=4] {'pix'}, use_global_device_ids=true, to_apply=%region_43.45 | all-reduce | flops 128 | bytes 1024 | tf_op jit(solution)/shard_map/psum | solution.py:58
  601.9 1.6 multiply_reduce_fusion.6
  603.5 17.1 %psum.201 = f32[128]{0:T(128)S(1)} all-reduce(f32[128]{0:T(128)S(1)} %get-tuple-element.354), channel_id=1, replica_groups=mesh['pix'=8,'frm'=4] {'pix'}, use_global_device_ids=true, to_apply=%region_45.47 | all-reduce | flops 128 | bytes 1024 | tf_op jit(solution)/shard_map/psum | solution.py:58
  621.3 1.6 multiply_reduce_fusion.5
  622.9 19.1 %psum.202 = f32[128]{0:T(128)S(1)} all-reduce(f32[128]{0:T(128)S(1)} %get-tuple-element.356), channel_id=1, replica_groups=mesh['pix'=8,'frm'=4] {'pix'}, use_global_device_ids=true, to_apply=%region_47.49 | all-reduce | flops 128 | bytes 1024 | tf_op jit(solution)/shard_map/psum | solution.py:58
  642.7 1.6 multiply_reduce_fusion.4
  644.3 17.1 %psum.203 = f32[128]{0:T(128)S(1)} all-reduce(f32[128]{0:T(128)S(1)} %get-tuple-element.358), channel_id=1, replica_groups=mesh['pix'=8,'frm'=4] {'pix'}, use_global_device_ids=true, to_apply=%region_49.51 | all-reduce | flops 128 | bytes 1024 | tf_op jit(solution)/shard_map/psum | solution.py:58
  662.1 1.6 multiply_reduce_fusion.3
  663.8 19.1 %psum.204 = f32[128]{0:T(128)S(1)} all-reduce(f32[128]{0:T(128)S(1)} %get-tuple-element.360), channel_id=1, replica_groups=mesh['pix'=8,'frm'=4] {'pix'}, use_global_device_ids=true, to_apply=%region_51.53 | all-reduce | flops 128 | bytes 1024 | tf_op jit(solution)/shard_map/psum | solution.py:58
  683.5 1.6 multiply_reduce_fusion.2
  685.1 17.1 %psum.205 = f32[128]{0:T(128)S(1)} all-reduce(f32[128]{0:T(128)S(1)} %get-tuple-element.362), channel_id=1, replica_groups=mesh['pix'=8,'frm'=4] {'pix'}, use_global_device_ids=true, to_apply=%region_53.55 | all-reduce | flops 128 | bytes 1024 | tf_op jit(solution)/shard_map/psum | solution.py:58
  703.0 1.6 multiply_reduce_fusion.1
  704.6 19.1 %psum.206 = f32[128]{0:T(128)S(1)} all-reduce(f32[128]{0:T(128)S(1)} %get-tuple-element.364), channel_id=1, replica_groups=mesh['pix'=8,'frm'=4] {'pix'}, use_global_device_ids=true, to_apply=%region_55.57 | all-reduce | flops 128 | bytes 1024 | tf_op jit(solution)/shard_map/psum | solution.py:58
  724.4 1.6 multiply_reduce_fusion
  726.0 17.1 %psum.207 = f32[128]{0:T(128)S(1)} all-reduce(f32[128]{0:T(128)S(1)} %get-tuple-element.366), channel_id=1, replica_groups=mesh['pix'=8,'frm'=4] {'pix'}, use_global_device_ids=true, to_apply=%region_57.59 | all-reduce | flops 128 | bytes 1024 | tf_op jit(solution)/shard_map/psum | solution.py:58
  743.4 3.2 scatter_custom_fusion
  (111 shorter events, 41.0 us)
Async XLA Ops:
  6.5 156.0 %copy-start.4 = (s32[1,256]{1,0:T(1,128)S(1)}, s32[1,256]{1,0:T(1,128)}, u32[]{:S(2)}) copy-start(s32[1,256]{1,0:T(1,128)} %param.59) | copy-start | bytes 3076
  6.5 156.2 %copy-start.3 = (s32[1024]{0:T(1024)S(1)}, s32[1024]{0:T(1024)}, u32[]{:S(2)}) copy-start(s32[1024]{0:T(1024)} %param.58) | copy-start | bytes 12292
  6.5 46.0 %all-gather.2.cloned.1.call-start = ((), (), s32[]{:S(2)}) async-start(), calls=%async_computation | async-start | bytes 1179648 | tf_op jit(solution)/shard_map/all_gather | solution.py:34
  7.3 83.4 %all-reduce.3.cloned.1.call-start = ((), (), s32[]{:S(2)}) async-start(), calls=%async_computation.1 | async-start | bytes 2097152 | tf_op jit(solution)/shard_map/psum | solution.py:38
  90.6 16.3 %collective-permute-start = (f32[128,1024]{1,0:T(8,128)}, f32[128,1024]{1,0:T(8,128)S(1)}, u32[]{:S(2)}, u32[]{:S(2)}) collective-permute-start(f32[128,1024]{1,0:T(8,128)} %get-tuple-element.294), channel_id=1, source_target_pairs={{0,4},{4,8},{8,12},{12,16},{16,20},{20,24},{24,28},{28,0},{1,5},{5... | collective-permute-start | bytes 1572872 | tf_op jit(solution)/shard_map/ppermute | solution.py:16
  106.9 15.2 %collective-permute-start.1 = (f32[128,1024]{1,0:T(8,128)S(1)}, f32[128,1024]{1,0:T(8,128)S(1)}, u32[]{:S(2)}, u32[]{:S(2)}) collective-permute-start(f32[128,1024]{1,0:T(8,128)S(1)} %collective-permute-done), channel_id=1, source_target_pairs={{0,4},{4,8},{8,12},{12,16},{16,20},{20,24},{24,28},{28,0},{1,5},{5... | collective-permute-start | bytes 1572872 | tf_op jit(solution)/shard_map/ppermute | solution.py:16
  122.1 14.3 %collective-permute-start.2 = (f32[128,1024]{1,0:T(8,128)S(1)}, f32[128,1024]{1,0:T(8,128)S(1)}, u32[]{:S(2)}, u32[]{:S(2)}) collective-permute-start(f32[128,1024]{1,0:T(8,128)S(1)} %collective-permute-done.1), channel_id=1, source_target_pairs={{0,4},{4,8},{8,12},{12,16},{16,20},{20,24},{24,28},{28,0},{1,5},{5... | collective-permute-start | bytes 1572872 | tf_op jit(solution)/shard_map/ppermute | solution.py:16
  136.4 13.5 %collective-permute-start.3 = (f32[128,1024]{1,0:T(8,128)S(1)}, f32[128,1024]{1,0:T(8,128)S(1)}, u32[]{:S(2)}, u32[]{:S(2)}) collective-permute-start(f32[128,1024]{1,0:T(8,128)S(1)} %collective-permute-done.2), channel_id=1, source_target_pairs={{0,4},{4,8},{8,12},{12,16},{16,20},{20,24},{24,28},{28,0},{1,5},{5... | collective-permute-start | bytes 1572872 | tf_op jit(solution)/shard_map/ppermute | solution.py:16
  149.9 12.6 %collective-permute-start.4 = (f32[128,1024]{1,0:T(8,128)S(1)}, f32[128,1024]{1,0:T(8,128)S(1)}, u32[]{:S(2)}, u32[]{:S(2)}) collective-permute-start(f32[128,1024]{1,0:T(8,128)S(1)} %collective-permute-done.3), channel_id=1, source_target_pairs={{0,4},{4,8},{8,12},{12,16},{16,20},{20,24},{24,28},{28,0},{1,5},{5... | collective-permute-start | bytes 1572872 | tf_op jit(solution)/shard_map/ppermute | solution.py:16
  162.5 12.3 %copy-start.1 = (f32[128,1024]{1,0:T(8,128)}, f32[128,1024]{1,0:T(8,128)S(1)}, u32[]{:S(2)}) copy-start(f32[128,1024]{1,0:T(8,128)S(1)} %collective-permute-done.4) | copy-start | bytes 1572868
  162.5 12.3 %collective-permute-start.5 = (f32[128,1024]{1,0:T(8,128)S(1)}, f32[128,1024]{1,0:T(8,128)}, u32[]{:S(2)}, u32[]{:S(2)}) collective-permute-start(f32[128,1024]{1,0:T(8,128)S(1)} %collective-permute-done.4), channel_id=1, source_target_pairs={{0,4},{4,8},{8,12},{12,16},{16,20},{20,24},{24,28},{28,0},{1,5},{5... | collective-permute-start | bytes 1572872 | tf_op jit(solution)/shard_map/ppermute | solution.py:16
  174.8 20.6 %collective-permute-start.6 = (f32[128,1024]{1,0:T(8,128)}, f32[128,1024]{1,0:T(8,128)}, u32[]{:S(2)}, u32[]{:S(2)}) collective-permute-start(f32[128,1024]{1,0:T(8,128)} %collective-permute-done.5), channel_id=1, source_target_pairs={{0,4},{4,8},{8,12},{12,16},{16,20},{20,24},{24,28},{28,0},{1,5},{5... | collective-permute-start | bytes 1572872 | tf_op jit(solution)/shard_map/ppermute | solution.py:16
  195.3 3.6 copy-start
  197.6 3.6 copy-start.2
Sparse Core Ops, SparseCore 0:
  9.5 42.9 all-gather.1
  55.5 35.0 all-reduce.2
